TPU v7x, 32 devices: a whole 2x2x4 slice. The times are simulated.
32 devices in a mesh: dp: 16 (over z, y, x), rep: 2 (over core).
Axes of the slice: x: 2, y: 2, z: 4, core: 2. Of those that a mesh axis runs over, the one named last changes fastest.
Arguments:
- queries: bfloat16 [2048, 2048], P(('dp', 'rep')), may hold values from -24 to 24
- documents: bfloat16 [2048, 2048], P(('dp', 'rep')), may hold values from -24 to 24
- partner: int32 [2048], P(('dp', 'rep')), may hold values from 0 to 2047, each once
Outputs:
- grad_queries: float32 [2048, 2048], P(('dp', 'rep'))
- grad_documents: float32 [2048, 2048], P(('dp', 'rep'))
Inputs may be any that keep to these rules, and one draw needn't show every extreme that they name: `partner`: every document index appears exactly once.
All inputs are finite; a program needn't handle non-finite values.
Results may differ from a plain program's by a relative error of at most 0.0031.
Values may be sent and summed in bfloat16 or wider, within the bound.
No kernel may reach another device: no remote copies, remote signals or barrier semaphores. Data moves between devices by JAX's collectives and lax.ppermute only.
A program may use at most 256 MiB of HBM per device.

v0:
```python
import jax
import jax.numpy as jnp
from jax import lax
from jax.sharding import PartitionSpec as P

WIDTHS = 9
logit_gain = 3.0


def merged(x, axis, combine):
    everything = jax.tree.map(lambda part: lax.all_gather(part, axis), x)
    leading = jax.tree.map(lambda part: part[0], everything)

    def hop(k, so_far):
        return combine(so_far, jax.tree.map(lambda part: part[k], everything))

    return lax.fori_loop(1, lax.axis_size(axis), hop, leading)


def contract(first_op, second_op):
    return lax.dot_general(
        first_op, second_op, (((1,), (1,)), ((), ())), preferred_element_type=jnp.float32
    )


def width_list(feature_dim):
    return [feature_dim >> WIDTHS - 1 - nested for nested in range(WIDTHS)]


def scores(first_op, second_op):
    uppers = width_list(first_op.shape[1])
    result = []
    running = jnp.zeros((first_op.shape[0], second_op.shape[0]), jnp.float32)
    lower_col = 0
    for upper_col in uppers:
        running = running + contract(
            first_op[:, lower_col:upper_col], second_op[:, lower_col:upper_col]
        )
        result.append(running * (logit_gain * upper_col ** (-0.5)))
        lower_col = upper_col
    return result


def band_sums(logit_list, total_list, target, uppers):
    bands = [None] * len(uppers)
    running = None
    for nested in reversed(range(len(uppers))):
        scale = logit_gain * uppers[nested] ** (-0.5)
        weight = (jnp.exp(logit_list[nested] - total_list[nested]) - target) * scale
        running = weight if running is None else running + weight
        bands[nested] = running.astype(jnp.bfloat16)
    return bands


def spread(bands, operand, uppers):
    pieces = []
    lower_col = 0
    for nested, upper_col in enumerate(uppers):
        block_part = operand[:, lower_col:upper_col]
        product = jnp.dot(bands[nested], block_part, preferred_element_type=jnp.float32)
        pieces.append(product)
        lower_col = upper_col
    return jnp.concatenate(pieces, axis=1)


def combine(first_pair, second_pair):
    biggest = jnp.maximum(first_pair[0], second_pair[0])
    return (
        biggest,
        first_pair[1] * jnp.exp(first_pair[0] - biggest)
        + second_pair[1] * jnp.exp(second_pair[0] - biggest),
    )


def on_device(queries, documents, partner):
    own_rows = queries.shape[0]
    uppers = width_list(queries.shape[1])
    rep_index = lax.axis_index("rep")
    dp_index = lax.axis_index("dp")
    rep_count = lax.axis_size("rep")
    every_rows = None
    every_partner = None
    every_rows, every_partner = (
        lax.all_gather(queries, ("dp", "rep"), axis=0, tiled=True),
        lax.all_gather(partner, ("dp", "rep"), axis=0, tiled=True),
    )
    pair_rows, pair_partner = (
        lax.all_gather(queries, "rep", axis=0, tiled=True),
        lax.all_gather(partner, "rep", axis=0, tiled=True),
    )
    partner_docs = lax.all_gather(documents, "dp", axis=0, tiled=True)
    col_pos = jnp.arange(partner_docs.shape[0], dtype=jnp.int32)
    col_ids = (col_pos // own_rows * rep_count + rep_index) * own_rows + col_pos % own_rows
    target = (pair_partner[:, None] == col_ids[None, :]).astype(jnp.float32)
    logit_list = scores(pair_rows, partner_docs)
    row_peaks = jnp.stack([jnp.max(logits, axis=1) for logits in logit_list])
    masses = jnp.stack(
        [
            jnp.sum(jnp.exp(logits - row_peaks[nested][:, None]), axis=1)
            for nested, logits in enumerate(logit_list)
        ]
    )
    row_peaks, masses = merged((row_peaks, masses), "rep", combine)
    totals = row_peaks + jnp.log(masses)
    bands = band_sums(
        logit_list, [totals[nested][:, None] for nested in range(len(uppers))], target, uppers
    )
    partial_queries = spread(bands, partner_docs, uppers)
    grad_queries = lax.psum_scatter(partial_queries, "rep", scatter_dimension=0, tiled=True)
    all_totals = lax.all_gather(totals, "dp", axis=1, tiled=True)
    own_ids = (dp_index * rep_count + rep_index) * own_rows + jnp.arange(own_rows, dtype=jnp.int32)
    own_target = (own_ids[:, None] == every_partner[None, :]).astype(jnp.float32)
    own_logits = scores(documents, every_rows)
    own_bands = band_sums(
        own_logits,
        [all_totals[nested][None, :] for nested in range(len(uppers))],
        own_target,
        uppers,
    )
    grad_documents = spread(own_bands, every_rows, uppers)
    return (grad_queries, grad_documents)


def solution(mesh):
    return jax.shard_map(
        on_device,
        mesh=mesh,
        in_specs=(P(("dp", "rep"), None), P(("dp", "rep"), None), P(("dp", "rep"))),
        out_specs=(P(("dp", "rep"), None), P(("dp", "rep"), None)),
        check_vma=False,
    )
```

profile of v0, /device:TPU:0, one launch (start us, length us, event | category | flops | bytes accessed | tf_op | source)
XLA Modules:
  0.0 192.3 jit_solution(15431763824458192233)
XLA Ops:
  7.2 0.7 all-gather.7.cloned.1.call-update
  7.9 0.7 all-gather.9.cloned.1.call-update
  8.7 1.2 dynamic-slice
  10.6 0.9 dynamic-update-slice
  11.5 0.8 dynamic-update-slice.1
  12.3 2.0 %all-reduce = s32[128]{0:T(128)S(1)} all-reduce(s32[128]{0:T(128)S(1)} %dynamic-update-slice), channel_id=1, replica_groups=mesh['dp'=16,'rep'=2] {'rep'}, use_global_device_ids=true, to_apply=%add | all-reduce | flops 128 | bytes 1024
  14.3 42.2 %all-reduce.1 = s32[2048]{0:T(1024)S(1)} all-reduce(s32[2048]{0:T(1024)S(1)} %dynamic-update-slice.1), channel_id=1, replica_groups=mesh['dp'=16,'rep'=2] {'dp','rep'}, use_global_device_ids=true, to_apply=%add.1 | all-reduce | flops 2048 | bytes 16384
  56.5 2.4 %all_gather.30 = bf16[128,2048]{1,0:T(8,128)(2,1)S(1)} all-gather(bf16[64,2048]{1,0:T(8,128)(2,1)} %param.3), channel_id=1, replica_groups=mesh['dp'=16,'rep'=2] {'rep'}, dimensions={0}, use_global_device_ids=true | all-gather | bytes 786432 | tf_op jit(solution)/shard_map/all_gather | solution.py:88
  58.9 30.3 %all-gather.7.cloned.1.call-done = bf16[1024,2048]{1,0:T(8,128)(2,1)} async-done(((bf16[64,2048]{1,0:T(8,128)(2,1)}), bf16[1024,2048]{1,0:T(8,128)(2,1)}) %all-gather.7.cloned.1.call-update) | async-done | bytes 4194320 | tf_op jit(solution)/shard_map/all_gather | solution.py:91
  89.2 1.4 multiply_reduce_fusion.7
  90.7 1.5 multiply_reduce_fusion.6
  92.2 1.3 multiply_reduce_fusion.5
  93.5 1.3 multiply_reduce_fusion.4
  94.9 0.4 multiply_reduce_fusion.3
  95.3 0.3 multiply_reduce_fusion.2
  95.6 1.2 multiply_reduce_fusion.1
  96.9 1.5 multiply_reduce_fusion
  98.4 2.0 %fusion.197 = (f32[128]{0:T(128)S(1)}, f32[128,1024]{1,0:T(8,128)S(1)}) fusion(f32[128,1024]{1,0:T(8,128)S(1)} %get-tuple-element.60, bf16[1024,2048]{1,0:T(8,128)(2,1)S(1)} %copy-done.1, bf16[128,2048]{1,0:T(8,128)(2,1)} %copy-done.8), kind=kOutput, calls=%fused_computation.231 | convolution fusion | flops 268828544 | bytes 3408384 | tf_op jit(solution)/shard_map/dot_general | solution.py:21
  102.7 1.9 %all-gather.3 = f32[2,9,128]{2,1,0:T(8,128)S(1)} all-gather(f32[1,9,128]{2,1,0:T(8,128)S(1)} %bitcast.79), channel_id=3, replica_groups=mesh['dp'=16,'rep'=2] {'rep'}, dimensions={0}, use_global_device_ids=true | all-gather | bytes 13824 | tf_op jit(solution)/shard_map/all_gather | solution.py:11
  104.6 1.8 all-gather.2
  106.5 2.2 %fusion.53 = (f32[128,1024]{1,0:T(8,128)S(1)}, f32[128,1024]{1,0:T(8,128)S(1)}, bf16[128,1024]{1,0:T(8,128)(2,1)S(1)}, f32[128,1024]{1,0:T(8,128)S(1)}) fusion(f32[128,1024]{1,0:T(8,128)S(1)} %get-tuple-element.50, f32[128]{0:T(128)S(1)} %get-tuple-element.38, s32[1024]{0:T(1024)S(1)} %fusion.177, s32[128]{0:T(128)S(1)} %all-reduce, ...), kind=kLoop, calls=%fused_computation.68 | loop fusion | flops 4718592 | bytes 5513216 | tf_op jit(solution)/shard_map/add | solution.py:50
  108.9 0.3 fusion.121
  109.6 0.4 fusion.119
  110.0 0.4 fusion.123
  110.4 0.4 fusion.95
  111.1 0.5 fusion.130
  111.7 0.6 fusion.25
  112.2 1.3 concatenate.6
  113.5 40.8 %all_gather.38 = f32[9,2048]{1,0:T(8,128)S(1)} all-gather(f32[9,128]{1,0:T(8,128)S(1)} %fusion.165), channel_id=1, replica_groups=mesh['dp'=16,'rep'=2] {'dp'}, dimensions={1}, use_global_device_ids=true | all-gather | bytes 78336 | tf_op jit(solution)/shard_map/all_gather | solution.py:110
  154.4 14.2 %all-gather.9.cloned.1.call-done = bf16[2048,2048]{1,0:T(8,128)(2,1)} async-done(((bf16[64,2048]{1,0:T(8,128)(2,1)}), bf16[2048,2048]{1,0:T(8,128)(2,1)}) %all-gather.9.cloned.1.call-update) | async-done | bytes 8388624 | tf_op jit(solution)/shard_map/all_gather | solution.py:84
  168.6 1.5 fusion.93
  170.1 1.7 convolution_add_fusion.6
  171.8 1.4 convolution_add_fusion.5
  173.2 1.4 convolution_add_fusion.4
  174.7 1.4 convolution_add_fusion.3
  176.1 1.3 convolution_add_fusion.2
  177.4 0.4 convolution_add_fusion.1
  177.9 0.8 convolution_add_fusion
  178.7 2.0 %fusion.70 = (f32[64,2048]{1,0:T(8,128)S(1)}, f32[64,2048]{1,0:T(8,128)S(1)}, f32[64,2048]{1,0:T(8,128)S(1)}, f32[64,2048]{1,0:T(8,128)S(1)}) fusion(f32[64,2048]{1,0:T(8,128)S(1)} %convolution_add_fusion.5, f32[2048]{0:T(1024)S(1)} %bitcast.84, s32[2048]{0:T(1024)S(1)} %all-reduce.1, s32[64]{0:T(128)S(1)} %iota_add_fusion, f32[2048]{0:T(1024)S(1)} %bitcast.77, ...), kind=kOutput, calls=%fused_computation.85 | convolution fusion | flops 273285120 | bytes 9634304 | tf_op jit(solution)/shard_map/dot_general | solution.py:21
  180.7 0.4 fusion.85
  181.0 0.4 fusion.79
  181.4 0.5 fusion.82
  181.9 0.5 fusion.88
  182.3 0.4 fusion.76
  183.0 0.5 fusion.91
  183.5 0.5 fusion.22
  184.1 0.8 fusion
  184.9 0.9 concatenate.7
  (47 shorter events, 3.7 us)
Async XLA Ops:
  7.2 82.1 %all-gather.7.cloned.1.call-start = ((), (), s32[]{:S(2)}) async-start(), calls=%async_computation.1 | async-start | bytes 4456448 | tf_op jit(solution)/shard_map/all_gather | solution.py:91
  7.9 160.7 %all-gather.9.cloned.1.call-start = ((), (), s32[]{:S(2)}) async-start(), calls=%async_computation.3 | async-start | bytes 8650752 | tf_op jit(solution)/shard_map/all_gather | solution.py:84
  8.6 177.2 %reduce-scatter.2.cloned.1.call-start = ((), (), s32[]{:S(2)}) async-start(), calls=%async_computation.2 | async-start | bytes 1572864 | tf_op jit(solution)/shard_map/reduce_scatter | solution.py:109
  58.9 36.8 %copy-start.8 = (bf16[128,2048]{1,0:T(8,128)(2,1)}, bf16[128,2048]{1,0:T(8,128)(2,1)S(1)}, u32[]{:S(2)}) copy-start(bf16[128,2048]{1,0:T(8,128)(2,1)S(1)} %all_gather.30) | copy-start | bytes 1572868
  89.2 5.7 %copy-start.1 = (bf16[1024,2048]{1,0:T(8,128)(2,1)S(1)}, bf16[1024,2048]{1,0:T(8,128)(2,1)}, u32[]{:S(2)}) copy-start(bf16[1024,2048]{1,0:T(8,128)(2,1)} %all-gather.7.cloned.1.call-done) | copy-start | bytes 12582916
  90.7 10.0 %copy-start.3 = (f32[128,1024]{1,0:T(8,128)}, f32[128,1024]{1,0:T(8,128)S(1)}, u32[]{:S(2)}) copy-start(f32[128,1024]{1,0:T(8,128)S(1)} %get-tuple-element.46) | copy-start | bytes 1572868
  98.4 4.0 %copy-start.5 = (f32[128,1024]{1,0:T(8,128)}, f32[128,1024]{1,0:T(8,128)S(1)}, u32[]{:S(2)}) copy-start(f32[128,1024]{1,0:T(8,128)S(1)} %get-tuple-element.60) | copy-start | bytes 1572868
  100.4 2.2 %copy-start.6 = (f32[128,1024]{1,0:T(8,128)}, f32[128,1024]{1,0:T(8,128)S(1)}, u32[]{:S(2)}) copy-start(f32[128,1024]{1,0:T(8,128)S(1)} %get-tuple-element.62) | copy-start | bytes 1572868
  102.7 6.0 %copy-start.2 = (bf16[1024,2048]{1,0:T(8,128)(2,1)S(1)}, bf16[1024,2048]{1,0:T(8,128)(2,1)}, u32[]{:S(2)}) copy-start(bf16[1024,2048]{1,0:T(8,128)(2,1)} %all-gather.7.cloned.1.call-done) | copy-start | bytes 12582916
  108.7 2.4 %copy-start.4 = (f32[128,1024]{1,0:T(8,128)S(1)}, f32[128,1024]{1,0:T(8,128)}, u32[]{:S(2)}) copy-start(f32[128,1024]{1,0:T(8,128)} %copy-done.3) | copy-start | bytes 1572868
  109.6 2.1 %copy-start.7 = (f32[128,1024]{1,0:T(8,128)S(1)}, f32[128,1024]{1,0:T(8,128)}, u32[]{:S(2)}) copy-start(f32[128,1024]{1,0:T(8,128)} %copy-done.6) | copy-start | bytes 1572868
  111.1 57.5 %copy-start.9 = (bf16[64,2048]{1,0:T(8,128)(2,1)S(1)}, bf16[64,2048]{1,0:T(8,128)(2,1)}, u32[]{:S(2)}) copy-start(bf16[64,2048]{1,0:T(8,128)(2,1)} %param.4) | copy-start | bytes 786436
  168.6 8.8 %copy-start = (bf16[2048,2048]{1,0:T(8,128)(2,1)S(1)}, bf16[2048,2048]{1,0:T(8,128)(2,1)}, u32[]{:S(2)}) copy-start(bf16[2048,2048]{1,0:T(8,128)(2,1)} %all-gather.9.cloned.1.call-done) | copy-start | bytes 25165828
Sparse Core Ops, SparseCore 0:
  10.7 78.4 all-gather.6
  92.1 76.4 all-gather.8
  171.4 7.1 reduce-scatter.1
where the time goes:
time: 193 us; the launch traced here: 192 us
  blocking collectives  91.1 us (47%)
  waiting for transfers between devices  46 us (24%)
  matrix products  30.8 us (16%)
  between operations  14.7 us (8%)
  local copies, waits for them, and re-layouts  5.31 us (3%)
  other arithmetic  4.33 us (2%)
    unnamed x2, blocking collectives  44.2 us
    all_gather x1, blocking collectives, on_device(): all_totals = lax.all_gather(totals, 'dp', axis=1, tiled=True)  40.8 us
    all_gather x1, waiting for transfers between devices, on_device(): partner_docs = lax.all_gather(documents, 'dp', axis=0, tiled=True)  30.3 us
    dot_general x18, matrix products, contract(): lax.dot_general(first_op, second_op, (((1,), (1,)), ((), ())), preferred_...  23.2 us
    all_gather x1, waiting for transfers between devices, on_device(): lax.all_gather(queries, ('dp', 'rep'), axis=0, tiled=True)  14.2 us
    dot_general x18, matrix products, spread(): jnp.dot(bands[nested], block_part, preferred_element_type=jnp.float32)  7.64 us
  transfers between devices with their start and end apart: 3, of which 2 were waited for; matrix products, arithmetic and copies ran while one was open for 21% of the time, Pallas kernels for 0%

commit v1 on v0

--- a/solution.py
+++ b/solution.py
@@ -5,6 +5,17 @@
 
 WIDTHS = 9
 logit_gain = 3.0
+
+
+def ring_gather(array, axis, dim):
+    ways = lax.axis_size(axis)
+    pieces = [array]
+    for far in range(1, ways):
+        pieces.append(
+            lax.ppermute(pieces[far - 1], axis, [(d, (d - 1) % ways) for d in range(ways)])
+        )
+    line = jnp.concatenate(pieces, axis=dim)
+    return jnp.roll(line, lax.axis_index(axis) * array.shape[dim], axis=dim)
 
 
 def merged(x, axis, combine):
@@ -107,7 +118,7 @@
     )
     partial_queries = spread(bands, partner_docs, uppers)
     grad_queries = lax.psum_scatter(partial_queries, "rep", scatter_dimension=0, tiled=True)
-    all_totals = lax.all_gather(totals, "dp", axis=1, tiled=True)
+    all_totals = ring_gather(totals, "dp", 1)
     own_ids = (dp_index * rep_count + rep_index) * own_rows + jnp.arange(own_rows, dtype=jnp.int32)
     own_target = (own_ids[:, None] == every_partner[None, :]).astype(jnp.float32)
     own_logits = scores(documents, every_rows)

time: 193 us -> 240 us (1.24)
  starting transfers between devices: 0.11 us -> 81.1 us
  blocking collectives: 91.1 us -> 50.3 us
  waiting for transfers between devices: 46 us -> 51.9 us
    ppermute x0 -> x15, starting transfers between devices: none -> 81 us  [ring_gather(): lax.ppermute(pieces[far - 1], axis, [(d, (d - 1) % ways) for d in range(w...]
    all_gather x1 -> x0, blocking collectives: 40.8 us -> none  [on_device(): all_totals = lax.all_gather(totals, 'dp', axis=1, tiled=True)]
    ppermute x0 -> x15, waiting for transfers between devices: none -> 20.1 us  [ring_gather(): lax.ppermute(pieces[far - 1], axis, [(d, (d - 1) % ways) for d in range(w...]
    all_gather x1, waiting for transfers between devices: 14.2 us -> 0.02 us  [on_device(): lax.all_gather(queries, ('dp', 'rep'), axis=0, tiled=True)]
  transfers between devices with their start and end apart: 3 -> 18, of which waited for: 2 -> 15; matrix products, arithmetic and copies ran while one was open for 21% -> 17% of each run, Pallas kernels for 0% -> 0%
where the time goes in v1:
time: 240 us; the launch traced here: 239 us
  starting transfers between devices  81.1 us (34%)
  waiting for transfers between devices  51.9 us (22%)
  blocking collectives  50.3 us (21%)
  matrix products  31 us (13%)
  between operations  14.9 us (6%)
  local copies, waits for them, and re-layouts  5.54 us (2%)
  other arithmetic  4.33 us (2%)
    ppermute x15, starting transfers between devices, ring_gather(): lax.ppermute(pieces[far - 1], axis, [(d, (d - 1) % ways) for d in range(w...  81 us
    unnamed x2, blocking collectives  44.2 us
    all_gather x1, waiting for transfers between devices, on_device(): partner_docs = lax.all_gather(documents, 'dp', axis=0, tiled=True)  30.3 us
    dot_general x18, matrix products, contract(): lax.dot_general(first_op, second_op, (((1,), (1,)), ((), ())), preferred_...  23.2 us
    ppermute x15, waiting for transfers between devices, ring_gather(): lax.ppermute(pieces[far - 1], axis, [(d, (d - 1) % ways) for d in range(w...  20.1 us
    dot_general x18, matrix products, spread(): jnp.dot(bands[nested], block_part, preferred_element_type=jnp.float32)  7.78 us
  transfers between devices with their start and end apart: 18, of which 15 were waited for; matrix products, arithmetic and copies ran while one was open for 17% of the time, Pallas kernels for 0%

profile of v1, /device:TPU:0, one launch (start us, length us, event | category | flops | bytes accessed | tf_op | source)
XLA Modules:
  0.0 238.9 jit_solution(7128253241492465353)
XLA Ops:
  12.3 2.0 all-reduce
  14.3 42.2 %all-reduce.1 = s32[2048]{0:T(1024)S(1)} all-reduce(s32[2048]{0:T(1024)S(1)} %dynamic-update-slice.1), channel_id=1, replica_groups=mesh['dp'=16,'rep'=2] {'dp','rep'}, use_global_device_ids=true, to_apply=%add.1 | all-reduce | flops 2048 | bytes 16384
  56.5 2.4 %all_gather.27 = bf16[128,2048]{1,0:T(8,128)(2,1)S(1)} all-gather(bf16[64,2048]{1,0:T(8,128)(2,1)} %param.3), channel_id=1, replica_groups=mesh['dp'=16,'rep'=2] {'rep'}, dimensions={0}, use_global_device_ids=true | all-gather | bytes 786432 | tf_op jit(solution)/shard_map/all_gather | solution.py:99
  58.9 30.3 %all-gather.7.cloned.1.call-done = bf16[1024,2048]{1,0:T(8,128)(2,1)} async-done(((bf16[64,2048]{1,0:T(8,128)(2,1)}), bf16[1024,2048]{1,0:T(8,128)(2,1)}) %all-gather.7.cloned.1.call-update) | async-done | bytes 4194320 | tf_op jit(solution)/shard_map/all_gather | solution.py:102
  89.2 1.4 multiply_reduce_fusion.7
  90.7 1.5 multiply_reduce_fusion.6
  92.2 1.4 multiply_reduce_fusion.5
  93.6 1.4 multiply_reduce_fusion.4
  96.9 1.5 multiply_reduce_fusion
  98.4 2.0 fusion.193
  102.7 1.9 all-gather.3
  104.6 1.8 all-gather.2
  106.5 2.9 %collective-permute-start = (f32[9,128]{1,0:T(8,128)S(1)}, f32[9,128]{1,0:T(8,128)S(1)}, u32[]{:S(2)}, u32[]{:S(2)}) collective-permute-start(f32[9,128]{1,0:T(8,128)S(1)} %get-tuple-element.24), channel_id=1, source_target_pairs={{0,30},{2,0},{4,2},{6,4},{8,6},{10,8},{12,10},{14,12},{16,14},{18,... | collective-permute-start | bytes 13832 | tf_op jit(solution)/shard_map/ppermute | solution.py:15
  109.3 2.2 fusion.41
  116.4 1.5 collective-permute-start.1
  117.9 2.2 collective-permute-done.1
  120.1 5.4 %collective-permute-start.2 = (f32[9,128]{1,0:T(8,128)S(1)}, f32[9,128]{1,0:T(8,128)S(1)}, u32[]{:S(2)}, u32[]{:S(2)}) collective-permute-start(f32[9,128]{1,0:T(8,128)S(1)} %collective-permute-done.1), channel_id=1, source_target_pairs={{0,30},{2,0},{4,2},{6,4},{8,6},{10,8},{12,10},{14,12},{16,14},{18,... | collective-permute-start | bytes 13832 | tf_op jit(solution)/shard_map/ppermute | solution.py:15
  125.5 1.4 collective-permute-done.2
  126.8 5.9 %collective-permute-start.3 = (f32[9,128]{1,0:T(8,128)S(1)}, f32[9,128]{1,0:T(8,128)S(1)}, u32[]{:S(2)}, u32[]{:S(2)}) collective-permute-start(f32[9,128]{1,0:T(8,128)S(1)} %collective-permute-done.2), channel_id=1, source_target_pairs={{0,30},{2,0},{4,2},{6,4},{8,6},{10,8},{12,10},{14,12},{16,14},{18,... | collective-permute-start | bytes 13832 | tf_op jit(solution)/shard_map/ppermute | solution.py:15
  132.7 1.4 collective-permute-done.3
  134.1 5.9 %collective-permute-start.4 = (f32[9,128]{1,0:T(8,128)S(1)}, f32[9,128]{1,0:T(8,128)S(1)}, u32[]{:S(2)}, u32[]{:S(2)}) collective-permute-start(f32[9,128]{1,0:T(8,128)S(1)} %collective-permute-done.3), channel_id=1, source_target_pairs={{0,30},{2,0},{4,2},{6,4},{8,6},{10,8},{12,10},{14,12},{16,14},{18,... | collective-permute-start | bytes 13832 | tf_op jit(solution)/shard_map/ppermute | solution.py:15
  140.0 1.5 collective-permute-done.4
  141.4 6.1 %collective-permute-start.5 = (f32[9,128]{1,0:T(8,128)S(1)}, f32[9,128]{1,0:T(8,128)S(1)}, u32[]{:S(2)}, u32[]{:S(2)}) collective-permute-start(f32[9,128]{1,0:T(8,128)S(1)} %collective-permute-done.4), channel_id=1, source_target_pairs={{0,30},{2,0},{4,2},{6,4},{8,6},{10,8},{12,10},{14,12},{16,14},{18,... | collective-permute-start | bytes 13832 | tf_op jit(solution)/shard_map/ppermute | solution.py:15
  147.6 1.5 collective-permute-done.5
  149.1 6.1 %collective-permute-start.6 = (f32[9,128]{1,0:T(8,128)S(1)}, f32[9,128]{1,0:T(8,128)S(1)}, u32[]{:S(2)}, u32[]{:S(2)}) collective-permute-start(f32[9,128]{1,0:T(8,128)S(1)} %collective-permute-done.5), channel_id=1, source_target_pairs={{0,30},{2,0},{4,2},{6,4},{8,6},{10,8},{12,10},{14,12},{16,14},{18,... | collective-permute-start | bytes 13832 | tf_op jit(solution)/shard_map/ppermute | solution.py:15
  155.2 1.4 collective-permute-done.6
  156.5 5.9 %collective-permute-start.7 = (f32[9,128]{1,0:T(8,128)S(1)}, f32[9,128]{1,0:T(8,128)S(1)}, u32[]{:S(2)}, u32[]{:S(2)}) collective-permute-start(f32[9,128]{1,0:T(8,128)S(1)} %collective-permute-done.6), channel_id=1, source_target_pairs={{0,30},{2,0},{4,2},{6,4},{8,6},{10,8},{12,10},{14,12},{16,14},{18,... | collective-permute-start | bytes 13832 | tf_op jit(solution)/shard_map/ppermute | solution.py:15
  162.4 1.4 collective-permute-done.7
  163.8 6.0 %collective-permute-start.8 = (f32[9,128]{1,0:T(8,128)S(1)}, f32[9,128]{1,0:T(8,128)S(1)}, u32[]{:S(2)}, u32[]{:S(2)}) collective-permute-start(f32[9,128]{1,0:T(8,128)S(1)} %collective-permute-done.7), channel_id=1, source_target_pairs={{0,30},{2,0},{4,2},{6,4},{8,6},{10,8},{12,10},{14,12},{16,14},{18,... | collective-permute-start | bytes 13832 | tf_op jit(solution)/shard_map/ppermute | solution.py:15
  169.8 1.4 collective-permute-done.8
  171.2 5.9 %collective-permute-start.9 = (f32[9,128]{1,0:T(8,128)S(1)}, f32[9,128]{1,0:T(8,128)S(1)}, u32[]{:S(2)}, u32[]{:S(2)}) collective-permute-start(f32[9,128]{1,0:T(8,128)S(1)} %collective-permute-done.8), channel_id=1, source_target_pairs={{0,30},{2,0},{4,2},{6,4},{8,6},{10,8},{12,10},{14,12},{16,14},{18,... | collective-permute-start | bytes 13832 | tf_op jit(solution)/shard_map/ppermute | solution.py:15
  177.1 1.4 collective-permute-done.9
  178.4 5.9 %collective-permute-start.10 = (f32[9,128]{1,0:T(8,128)S(1)}, f32[9,128]{1,0:T(8,128)S(1)}, u32[]{:S(2)}, u32[]{:S(2)}) collective-permute-start(f32[9,128]{1,0:T(8,128)S(1)} %collective-permute-done.9), channel_id=1, source_target_pairs={{0,30},{2,0},{4,2},{6,4},{8,6},{10,8},{12,10},{14,12},{16,14},{18,... | collective-permute-start | bytes 13832 | tf_op jit(solution)/shard_map/ppermute | solution.py:15
  184.3 1.4 collective-permute-done.10
  185.7 5.9 %collective-permute-start.11 = (f32[9,128]{1,0:T(8,128)S(1)}, f32[9,128]{1,0:T(8,128)S(1)}, u32[]{:S(2)}, u32[]{:S(2)}) collective-permute-start(f32[9,128]{1,0:T(8,128)S(1)} %collective-permute-done.10), channel_id=1, source_target_pairs={{0,30},{2,0},{4,2},{6,4},{8,6},{10,8},{12,10},{14,12},{16,14},{18,... | collective-permute-start | bytes 13832 | tf_op jit(solution)/shard_map/ppermute | solution.py:15
  191.6 1.4 collective-permute-done.11
  192.9 5.9 %collective-permute-start.12 = (f32[9,128]{1,0:T(8,128)S(1)}, f32[9,128]{1,0:T(8,128)S(1)}, u32[]{:S(2)}, u32[]{:S(2)}) collective-permute-start(f32[9,128]{1,0:T(8,128)S(1)} %collective-permute-done.11), channel_id=1, source_target_pairs={{0,30},{2,0},{4,2},{6,4},{8,6},{10,8},{12,10},{14,12},{16,14},{18,... | collective-permute-start | bytes 13832 | tf_op jit(solution)/shard_map/ppermute | solution.py:15
  198.8 1.4 collective-permute-done.12
  200.2 5.9 %collective-permute-start.13 = (f32[9,128]{1,0:T(8,128)S(1)}, f32[9,128]{1,0:T(8,128)S(1)}, u32[]{:S(2)}, u32[]{:S(2)}) collective-permute-start(f32[9,128]{1,0:T(8,128)S(1)} %collective-permute-done.12), channel_id=1, source_target_pairs={{0,30},{2,0},{4,2},{6,4},{8,6},{10,8},{12,10},{14,12},{16,14},{18,... | collective-permute-start | bytes 13832 | tf_op jit(solution)/shard_map/ppermute | solution.py:15
  206.0 1.4 collective-permute-done.13
  207.4 5.9 %collective-permute-start.14 = (f32[9,128]{1,0:T(8,128)S(1)}, f32[9,128]{1,0:T(8,128)S(1)}, u32[]{:S(2)}, u32[]{:S(2)}) collective-permute-start(f32[9,128]{1,0:T(8,128)S(1)} %collective-permute-done.13), channel_id=1, source_target_pairs={{0,30},{2,0},{4,2},{6,4},{8,6},{10,8},{12,10},{14,12},{16,14},{18,... | collective-permute-start | bytes 13832 | tf_op jit(solution)/shard_map/ppermute | solution.py:15
  213.3 1.4 collective-permute-done.14
  215.1 1.5 fusion.82
  216.6 1.7 convolution_add_fusion.6
  218.3 1.4 convolution_add_fusion.5
  219.7 1.4 convolution_add_fusion.4
  221.1 1.4 convolution_add_fusion.3
  225.1 2.0 fusion.59
  (107 shorter events, 21.5 us)
Async XLA Ops:
  7.2 82.1 %all-gather.7.cloned.1.call-start = ((), (), s32[]{:S(2)}) async-start(), calls=%async_computation.1 | async-start | bytes 4456448 | tf_op jit(solution)/shard_map/all_gather | solution.py:102
  7.9 207.1 %all-gather.9.cloned.1.call-start = ((), (), s32[]{:S(2)}) async-start(), calls=%async_computation.3 | async-start | bytes 8650752 | tf_op jit(solution)/shard_map/all_gather | solution.py:95
  8.6 223.8 %reduce-scatter.2.cloned.1.call-start = ((), (), s32[]{:S(2)}) async-start(), calls=%async_computation.2 | async-start | bytes 1572864 | tf_op jit(solution)/shard_map/reduce_scatter | solution.py:120
  58.9 36.7 %copy-start.8 = (bf16[128,2048]{1,0:T(8,128)(2,1)}, bf16[128,2048]{1,0:T(8,128)(2,1)S(1)}, u32[]{:S(2)}) copy-start(bf16[128,2048]{1,0:T(8,128)(2,1)S(1)} %all_gather.27) | copy-start | bytes 1572868
  89.2 5.7 %copy-start.1 = (bf16[1024,2048]{1,0:T(8,128)(2,1)S(1)}, bf16[1024,2048]{1,0:T(8,128)(2,1)}, u32[]{:S(2)}) copy-start(bf16[1024,2048]{1,0:T(8,128)(2,1)} %all-gather.7.cloned.1.call-done) | copy-start | bytes 12582916
  90.7 10.0 %copy-start.3 = (f32[128,1024]{1,0:T(8,128)}, f32[128,1024]{1,0:T(8,128)S(1)}, u32[]{:S(2)}) copy-start(f32[128,1024]{1,0:T(8,128)S(1)} %get-tuple-element.48) | copy-start | bytes 1572868
  98.4 4.0 %copy-start.5 = (f32[128,1024]{1,0:T(8,128)}, f32[128,1024]{1,0:T(8,128)S(1)}, u32[]{:S(2)}) copy-start(f32[128,1024]{1,0:T(8,128)S(1)} %get-tuple-element.62) | copy-start | bytes 1572868
  100.4 2.2 copy-start.6
  102.7 8.8 %copy-start.2 = (bf16[1024,2048]{1,0:T(8,128)(2,1)S(1)}, bf16[1024,2048]{1,0:T(8,128)(2,1)}, u32[]{:S(2)}) copy-start(bf16[1024,2048]{1,0:T(8,128)(2,1)} %all-gather.7.cloned.1.call-done) | copy-start | bytes 12582916
  106.5 9.9 %collective-permute-start = (f32[9,128]{1,0:T(8,128)S(1)}, f32[9,128]{1,0:T(8,128)S(1)}, u32[]{:S(2)}, u32[]{:S(2)}) collective-permute-start(f32[9,128]{1,0:T(8,128)S(1)} %get-tuple-element.24), channel_id=1, source_target_pairs={{0,30},{2,0},{4,2},{6,4},{8,6},{10,8},{12,10},{14,12},{16,14},{18,... | collective-permute-start | bytes 13832 | tf_op jit(solution)/shard_map/ppermute | solution.py:15
  111.5 2.2 copy-start.4
  112.2 2.1 copy-start.7
  114.2 100.8 %copy-start.9 = (bf16[64,2048]{1,0:T(8,128)(2,1)S(1)}, bf16[64,2048]{1,0:T(8,128)(2,1)}, u32[]{:S(2)}) copy-start(bf16[64,2048]{1,0:T(8,128)(2,1)} %param.4) | copy-start | bytes 786436
  116.4 3.7 %collective-permute-start.1 = (f32[9,128]{1,0:T(8,128)S(1)}, f32[9,128]{1,0:T(8,128)S(1)}, u32[]{:S(2)}, u32[]{:S(2)}) collective-permute-start(f32[9,128]{1,0:T(8,128)S(1)} %collective-permute-done), channel_id=1, source_target_pairs={{0,30},{2,0},{4,2},{6,4},{8,6},{10,8},{12,10},{14,12},{16,14},{18,... | collective-permute-start | bytes 13832 | tf_op jit(solution)/shard_map/ppermute | solution.py:15
  120.1 6.7 %collective-permute-start.2 = (f32[9,128]{1,0:T(8,128)S(1)}, f32[9,128]{1,0:T(8,128)S(1)}, u32[]{:S(2)}, u32[]{:S(2)}) collective-permute-start(f32[9,128]{1,0:T(8,128)S(1)} %collective-permute-done.1), channel_id=1, source_target_pairs={{0,30},{2,0},{4,2},{6,4},{8,6},{10,8},{12,10},{14,12},{16,14},{18,... | collective-permute-start | bytes 13832 | tf_op jit(solution)/shard_map/ppermute | solution.py:15
  126.8 7.2 %collective-permute-start.3 = (f32[9,128]{1,0:T(8,128)S(1)}, f32[9,128]{1,0:T(8,128)S(1)}, u32[]{:S(2)}, u32[]{:S(2)}) collective-permute-start(f32[9,128]{1,0:T(8,128)S(1)} %collective-permute-done.2), channel_id=1, source_target_pairs={{0,30},{2,0},{4,2},{6,4},{8,6},{10,8},{12,10},{14,12},{16,14},{18,... | collective-permute-start | bytes 13832 | tf_op jit(solution)/shard_map/ppermute | solution.py:15
  134.1 7.3 %collective-permute-start.4 = (f32[9,128]{1,0:T(8,128)S(1)}, f32[9,128]{1,0:T(8,128)S(1)}, u32[]{:S(2)}, u32[]{:S(2)}) collective-permute-start(f32[9,128]{1,0:T(8,128)S(1)} %collective-permute-done.3), channel_id=1, source_target_pairs={{0,30},{2,0},{4,2},{6,4},{8,6},{10,8},{12,10},{14,12},{16,14},{18,... | collective-permute-start | bytes 13832 | tf_op jit(solution)/shard_map/ppermute | solution.py:15
  141.4 7.6 %collective-permute-start.5 = (f32[9,128]{1,0:T(8,128)S(1)}, f32[9,128]{1,0:T(8,128)S(1)}, u32[]{:S(2)}, u32[]{:S(2)}) collective-permute-start(f32[9,128]{1,0:T(8,128)S(1)} %collective-permute-done.4), channel_id=1, source_target_pairs={{0,30},{2,0},{4,2},{6,4},{8,6},{10,8},{12,10},{14,12},{16,14},{18,... | collective-permute-start | bytes 13832 | tf_op jit(solution)/shard_map/ppermute | solution.py:15
  149.1 7.5 %collective-permute-start.6 = (f32[9,128]{1,0:T(8,128)S(1)}, f32[9,128]{1,0:T(8,128)S(1)}, u32[]{:S(2)}, u32[]{:S(2)}) collective-permute-start(f32[9,128]{1,0:T(8,128)S(1)} %collective-permute-done.5), channel_id=1, source_target_pairs={{0,30},{2,0},{4,2},{6,4},{8,6},{10,8},{12,10},{14,12},{16,14},{18,... | collective-permute-start | bytes 13832 | tf_op jit(solution)/shard_map/ppermute | solution.py:15
  156.5 7.2 %collective-permute-start.7 = (f32[9,128]{1,0:T(8,128)S(1)}, f32[9,128]{1,0:T(8,128)S(1)}, u32[]{:S(2)}, u32[]{:S(2)}) collective-permute-start(f32[9,128]{1,0:T(8,128)S(1)} %collective-permute-done.6), channel_id=1, source_target_pairs={{0,30},{2,0},{4,2},{6,4},{8,6},{10,8},{12,10},{14,12},{16,14},{18,... | collective-permute-start | bytes 13832 | tf_op jit(solution)/shard_map/ppermute | solution.py:15
  163.8 7.4 %collective-permute-start.8 = (f32[9,128]{1,0:T(8,128)S(1)}, f32[9,128]{1,0:T(8,128)S(1)}, u32[]{:S(2)}, u32[]{:S(2)}) collective-permute-start(f32[9,128]{1,0:T(8,128)S(1)} %collective-permute-done.7), channel_id=1, source_target_pairs={{0,30},{2,0},{4,2},{6,4},{8,6},{10,8},{12,10},{14,12},{16,14},{18,... | collective-permute-start | bytes 13832 | tf_op jit(solution)/shard_map/ppermute | solution.py:15
  171.2 7.2 %collective-permute-start.9 = (f32[9,128]{1,0:T(8,128)S(1)}, f32[9,128]{1,0:T(8,128)S(1)}, u32[]{:S(2)}, u32[]{:S(2)}) collective-permute-start(f32[9,128]{1,0:T(8,128)S(1)} %collective-permute-done.8), channel_id=1, source_target_pairs={{0,30},{2,0},{4,2},{6,4},{8,6},{10,8},{12,10},{14,12},{16,14},{18,... | collective-permute-start | bytes 13832 | tf_op jit(solution)/shard_map/ppermute | solution.py:15
  178.4 7.2 %collective-permute-start.10 = (f32[9,128]{1,0:T(8,128)S(1)}, f32[9,128]{1,0:T(8,128)S(1)}, u32[]{:S(2)}, u32[]{:S(2)}) collective-permute-start(f32[9,128]{1,0:T(8,128)S(1)} %collective-permute-done.9), channel_id=1, source_target_pairs={{0,30},{2,0},{4,2},{6,4},{8,6},{10,8},{12,10},{14,12},{16,14},{18,... | collective-permute-start | bytes 13832 | tf_op jit(solution)/shard_map/ppermute | solution.py:15
  185.7 7.2 %collective-permute-start.11 = (f32[9,128]{1,0:T(8,128)S(1)}, f32[9,128]{1,0:T(8,128)S(1)}, u32[]{:S(2)}, u32[]{:S(2)}) collective-permute-start(f32[9,128]{1,0:T(8,128)S(1)} %collective-permute-done.10), channel_id=1, source_target_pairs={{0,30},{2,0},{4,2},{6,4},{8,6},{10,8},{12,10},{14,12},{16,14},{18,... | collective-permute-start | bytes 13832 | tf_op jit(solution)/shard_map/ppermute | solution.py:15
  192.9 7.2 %collective-permute-start.12 = (f32[9,128]{1,0:T(8,128)S(1)}, f32[9,128]{1,0:T(8,128)S(1)}, u32[]{:S(2)}, u32[]{:S(2)}) collective-permute-start(f32[9,128]{1,0:T(8,128)S(1)} %collective-permute-done.11), channel_id=1, source_target_pairs={{0,30},{2,0},{4,2},{6,4},{8,6},{10,8},{12,10},{14,12},{16,14},{18,... | collective-permute-start | bytes 13832 | tf_op jit(solution)/shard_map/ppermute | solution.py:15
  200.2 7.2 %collective-permute-start.13 = (f32[9,128]{1,0:T(8,128)S(1)}, f32[9,128]{1,0:T(8,128)S(1)}, u32[]{:S(2)}, u32[]{:S(2)}) collective-permute-start(f32[9,128]{1,0:T(8,128)S(1)} %collective-permute-done.12), channel_id=1, source_target_pairs={{0,30},{2,0},{4,2},{6,4},{8,6},{10,8},{12,10},{14,12},{16,14},{18,... | collective-permute-start | bytes 13832 | tf_op jit(solution)/shard_map/ppermute | solution.py:15
  207.4 7.2 %collective-permute-start.14 = (f32[9,128]{1,0:T(8,128)S(1)}, f32[9,128]{1,0:T(8,128)S(1)}, u32[]{:S(2)}, u32[]{:S(2)}) collective-permute-start(f32[9,128]{1,0:T(8,128)S(1)} %collective-permute-done.13), channel_id=1, source_target_pairs={{0,30},{2,0},{4,2},{6,4},{8,6},{10,8},{12,10},{14,12},{16,14},{18,... | collective-permute-start | bytes 13832 | tf_op jit(solution)/shard_map/ppermute | solution.py:15
  215.1 8.8 %copy-start = (bf16[2048,2048]{1,0:T(8,128)(2,1)S(1)}, bf16[2048,2048]{1,0:T(8,128)(2,1)}, u32[]{:S(2)}) copy-start(bf16[2048,2048]{1,0:T(8,128)(2,1)} %all-gather.9.cloned.1.call-done) | copy-start | bytes 25165828
Sparse Core Ops, SparseCore 0:
  10.7 78.4 all-gather.6
  92.1 76.6 all-gather.8
  171.6 6.7 reduce-scatter.1
